TPU v7x, 32 devices: a whole 2x2x4 slice. The times are simulated.
32 devices in a mesh: gx: 4 (over y, core), gy: 4 (over z), gz: 2 (over x).
Axes of the slice: x: 2, y: 2, z: 4, core: 2. Of those that a mesh axis runs over, the one named last changes fastest.
Arguments:
- a_vals: float32 [4, 8, 2, 6, 128, 128], P('gy', 'gx', 'gz'), may hold values from -0.25 to 0.25
- a_cols: int32 [4, 8, 2, 6], P('gy', 'gx', 'gz'), may hold values from 0 to 15, as said below
- a_count: int32 [4, 8, 2], P('gy', 'gx', 'gz'), may hold values from 1 to 6, as said below
- p_vals: float32 [2, 16, 4, 1, 128, 128], P('gz', 'gy', 'gx'), may hold values from -6 to 6
- p_cols: int32 [2, 16, 4, 1], P('gz', 'gy', 'gx'), may hold values from 0 to 1, as said below
- p_count: int32 [2, 16, 4], P('gz', 'gy', 'gx'), may hold values from 0 to 1, as said below
Outputs:
- c_tiles: float32 [4096, 1024], P(('gy', 'gz'), 'gx')
Inputs may be any that keep to these rules, and one draw needn't show every extreme that they name: `a_cols`: inner tile indices of one block row and slice are distinct across its 6 slots. Slots 0 to a_count - 1 are live; the block rows of every device include one with all 6 slots live. `p_cols`: column tiles of one block row and group are distinct across its 1 slots. Slots 0 to p_count - 1 are live; the block rows of every device include one with all 1 slots live.
All inputs are finite; a program needn't handle non-finite values.
Results may differ from a plain program's by a relative error of at most 0.0003.
Values sent between devices are 32-bit elements; how exact they have to be, the bound alone decides.
A program may use at most 128 MiB of HBM per device.

v0:
```python
import functools

import jax
import jax.numpy as jnp
from jax import lax
from jax.experimental import pallas as pl
from jax.experimental.pallas import tpu as pltpu
from jax.sharding import PartitionSpec as P

COLS_DEV = 2
MESH = pl.DeviceIdType.MESH


def kernel(
    gx, gy, gz, slots_p,
    a_ref, p_ref, ac_ref, an_ref, pc_ref, pn_ref, o_ref,
    a_all, p_own, p_all, ma, mp, sa, sp, p_mul, c_send, c_recv,
    a_recv, a_sy, a_sp, a_sf, p_load, p_recv, p_send,
    ma_recv, ma_send, mp_recv, mp_send, s_sem, c_rs, c_ss,
):
    rows, slots, tile = a_ref.shape[0], a_ref.shape[1], a_ref.shape[2]
    tiles_p = p_ref.shape[0]
    inner = tiles_p // slots_p
    pairs = p_all.shape[2]
    rows_all = gx * rows
    rows_out = rows_all // gz
    zero_tile = gy * inner
    half = tile // 2
    cuts_a = a_recv.shape[2]
    part_a = slots // cuts_a
    me_x, me_y, me_z = lax.axis_index("gx"), lax.axis_index("gy"), lax.axis_index("gz")
    chips = gx // 2
    chip, core = me_x // 2, me_x % 2
    partner = chip * 2 + (1 - core)

    barrier = pltpu.get_barrier_semaphore()
    for name, size, me in (("gx", gx, me_x), ("gy", gy, me_y), ("gz", gz, me_z)):
        for d in range(1, size):
            pl.semaphore_signal(
                barrier, inc=1, device_id={name: lax.rem(me + d, size)}, device_id_type=MESH
            )
    load = pltpu.make_async_copy(p_ref, p_own, p_load)
    load.start()
    for r in range(rows):
        for h in range(cuts_a):
            cut = pl.ds(h * part_a, part_a)
            pltpu.make_async_copy(
                a_ref.at[r, cut], a_all.at[me_x, r, cut], a_recv.at[me_x, r, h]).start()

    line = lax.broadcasted_iota(jnp.int32, (8, 128), 0)
    lane = lax.broadcasted_iota(jnp.int32, (8, 128), 1)
    meta = jnp.zeros((8, 128), jnp.int32)
    for r in range(rows):
        for s in range(slots):
            pick = jnp.where(s < an_ref[r], ac_ref[0, r, 0, s], zero_tile)
            meta = jnp.where((line == 0) & (lane == r * slots + s), pick, meta)
    for t in range(tiles_p):
        code = jnp.where(t % slots_p < pn_ref[t // slots_p], pc_ref[t], -1)
        meta = jnp.where((line == 1) & (lane == t), code, meta)
    ma[me_x] = meta
    mp[me_y] = meta
    p_mul[0, zero_tile] = jnp.zeros_like(p_mul[0, zero_tile])
    p_mul[1, zero_tile] = jnp.zeros_like(p_mul[1, zero_tile])

    left = lax.broadcasted_iota(jnp.int32, (tile, tile), 1) < half
    load.wait()
    for j in range(pairs):
        one, two = p_own[2 * j], p_own[min(2 * j + 1, tiles_p - 1)]
        p_all[me_y, 0, j] = jnp.where(left, one, pltpu.roll(two, half, 1))
        p_all[me_y, 1, j] = jnp.where(left, pltpu.roll(one, half, 1), two)

    pl.semaphore_wait(barrier, gx + gy + gz - 3)

    def remote(src, dst, send, recv, where):
        return pltpu.make_async_remote_copy(
            src_ref=src, dst_ref=dst, send_sem=send, recv_sem=recv,
            device_id=where, device_id_type=MESH)

    sends = []
    for d in range(1, gx):
        sends.append(remote(ma.at[me_x], ma.at[me_x], ma_send.at[d], ma_recv.at[me_x],
                            {"gx": lax.rem(me_x + d, gx)}))
    for d in range(1, gy):
        sends.append(remote(mp.at[me_y], mp.at[me_y], mp_send.at[d], mp_recv.at[me_y],
                            {"gy": lax.rem(me_y + d, gy)}))
    for r in range(rows):
        for h in range(cuts_a):
            cut = pl.ds(h * part_a, part_a)
            for d in range(1, chips):
                sends.append(remote(
                    a_ref.at[r, cut], a_all.at[me_x, r, cut], a_sy.at[d, r, h],
                    a_recv.at[me_x, r, h], {"gx": lax.rem(chip + d, chips) * 2 + core}))
            sends.append(remote(
                a_ref.at[r, cut], a_all.at[me_x, r, cut], a_sp.at[r, h],
                a_recv.at[me_x, r, h], {"gx": partner}))
    for copy in sends:
        copy.start()

    def p_copy(side, src, h, j):
        ref = p_all.at[src, h, j]
        step = 1 if side == 0 else -1
        return remote(ref, ref, p_send.at[side, src, h, j], p_recv.at[src, h, j],
                      {"gy": lax.rem(me_y + step + gy, gy)})

    has_next = (me_y + 1 < gy, me_y >= 1)

    def send_own(h):
        for j in range(pairs):
            for side in (0, 1):
                @pl.when(has_next[side])
                def _(side=side, j=j):
                    p_copy(side, me_y, h, j).start()

    send_own(0)

    def wait_a(g, r, h):
        ref = a_all.at[g, r, pl.ds(h * part_a, part_a)]
        pltpu.make_async_copy(ref, ref, a_recv.at[g, r, h]).wait()

    for d in range(1, gx):
        g = lax.rem(me_x + d, gx)
        pltpu.make_async_copy(ma.at[g], ma.at[g], ma_recv.at[g]).wait()
    for d in range(1, gy):
        g = lax.rem(me_y + d, gy)
        pltpu.make_async_copy(mp.at[g], mp.at[g], mp_recv.at[g]).wait()
    moves = [pltpu.make_async_copy(ma, sa, s_sem.at[0]), pltpu.make_async_copy(mp, sp, s_sem.at[1])]
    for copy in moves:
        copy.start()
    for copy in moves:
        copy.wait()

    side_of_lane = lax.broadcasted_iota(jnp.int32, (tile, tile), 1) // half

    def split(src, h):
        def one(k, carry):
            value = jnp.zeros((tile, tile), jnp.float32)
            for s in range(slots_p):
                t = k * slots_p + s
                code = sp[src, 1, t]
                packed = p_all[src, h, t // 2]
                turned = pltpu.roll(packed, half, 1)
                placed = jnp.where(code == t % 2, packed, turned)
                value = value + jnp.where(side_of_lane == code, placed, 0.0)
            high = value.astype(jnp.bfloat16)
            low = (value - high.astype(jnp.float32)).astype(jnp.bfloat16)
            p_mul[h, src * inner + k, :, :tile] = high
            p_mul[h, src * inner + k, :, tile:] = low
            return carry

        lax.fori_loop(0, inner, one, 0)

    def relay_copy(d, r, h):
        src = lax.rem(chip - d + chips, chips) * 2 + core
        ref = a_all.at[src, r, pl.ds(h * part_a, part_a)]
        return src, remote(ref, ref, a_sf.at[d, r, h], a_recv.at[src, r, h], {"gx": partner})

    def relay(d, r, h):
        src, copy = relay_copy(d, r, h)
        wait_a(src, r, h)
        copy.start()

    def source(side, d):
        src = me_y - d if side == 0 else me_y + d
        return src, src >= 0 if side == 0 else src < gy

    def gather_half(h, relays):
        done = 0
        for d in range(1, gy):
            for side in (0, 1):
                src, there = source(side, d)

                @pl.when(there)
                def _(src=src, side=side):
                    for j in range(pairs):
                        ref = p_all.at[src, h, j]
                        pltpu.make_async_copy(ref, ref, p_recv.at[src, h, j]).wait()

                        @pl.when(has_next[side])
                        def _(j=j):
                            p_copy(side, src, h, j).start()

                    split(src, h)
            if h == 0 and d == max(gy - 2, 1):
                send_own(1)
            goal = max(0, d - 1) * len(relays) // (gy - 1)
            while done < goal:
                relay(*relays[done])
                done += 1
        while done < len(relays):
            relay(*relays[done])
            done += 1

    relays = [(d, r, h) for r in range(rows) for h in range(cuts_a) for d in range(1, chips)]

    def product(q, h):
        g, r = q // rows, lax.rem(q, rows)
        picks = [sa[g, 0, r * slots + s] for s in range(slots)]
        values = jnp.concatenate([a_all[g, r, s] for s in range(slots)], axis=1)
        high = values.astype(jnp.bfloat16)
        low = (values - high.astype(jnp.float32)).astype(jnp.bfloat16)
        right = jnp.concatenate([p_mul[h, i] for i in picks], axis=0)
        out = jnp.dot(jnp.concatenate([high, low], axis=0), right,
                      preferred_element_type=jnp.float32)
        return out[:tile, :tile] + (out[:tile, tile:] + out[tile:, :tile] + out[tile:, tile:])

    def await_row(q):
        g, r = q // rows, lax.rem(q, rows)
        mine = jnp.logical_and(g % 2 == core, g // 2 != chip)

        @pl.when(jnp.logical_not(mine))
        def _():
            for h in range(cuts_a):
                wait_a(g, r, h)

    def c_copy(d, i, h):
        return remote(c_send.at[d, i, h], c_recv.at[d, i, h], c_ss.at[d, i, h],
                      c_rs.at[d, i, h], {"gz": lax.rem(me_z + d, gz)})

    def send_rows(lines, halves, first):
        for d in range(1, gz):
            def send_row(n, carry, d=d):
                i = lines[0] + n * (lines[1] - lines[0] if len(lines) > 1 else 1)
                q = lax.rem(me_z + d, gz) * rows_out + i
                if first:
                    await_row(q)
                for h in halves:
                    c_send[d, i, h] = product(q, h)
                    c_copy(d, i, h).start()
                return carry

            lax.fori_loop(0, len(lines), send_row, 0)

    early = list(range(0, rows_out, rows))
    split(me_y, 0)
    gather_half(0, [x for x in relays if x[1] == 0])
    send_rows(early, (0,), True)
    split(me_y, 1)
    gather_half(1, [x for x in relays if x[1] > 0])
    send_rows(early, (1,), False)
    for r in range(1, rows):
        late = list(range(r, rows_out, rows))
        if late:
            send_rows(late, (0, 1), True)

    def own_row(i, carry):
        q = me_z * rows_out + i
        await_row(q)
        for h in (0, 1):
            c_send[0, i, h] = product(q, h)
        return carry

    lax.fori_loop(0, rows_out, own_row, 0)

    def finish(i):
        halves = []
        for h in (0, 1):
            value = c_send[0, i, h]
            for d in range(1, gz):
                ref = c_recv.at[d, i, h]
                pltpu.make_async_copy(ref, ref, c_rs.at[d, i, h]).wait()
                value = value + c_recv[d, i, h]
            halves.append(value)
        one, two = halves
        at = pl.ds(i * tile, tile)
        o_ref[at, :tile] = jnp.where(left, one, pltpu.roll(two, half, 1))
        o_ref[at, tile:] = jnp.where(left, pltpu.roll(one, half, 1), two)

    for r in range(rows):
        for i in range(r, rows_out, rows):
            finish(i)

    for copy in sends:
        copy.wait_send()
    for d, r, h in relays:
        relay_copy(d, r, h)[1].wait_send()
    for side in (0, 1):
        for d in range(0, gy):
            src, there = source(side, d)

            @pl.when(jnp.logical_and(there, has_next[side]))
            def _(src=src, side=side):
                for h in (0, 1):
                    for j in range(pairs):
                        p_copy(side, src, h, j).wait_send()
    for d in range(1, gz):
        for i in range(rows_out):
            for h in (0, 1):
                c_copy(d, i, h).wait_send()


def body(gx, gy, gz, a_vals, a_cols, a_count, p_vals, p_cols, p_count):
    rows, slots, tile = a_vals.shape[1], a_vals.shape[3], a_vals.shape[-1]
    inner, slots_p = p_vals.shape[1], p_vals.shape[3]
    tiles_p = inner * slots_p
    pairs = (tiles_p + 1) // 2
    rows_out = gx * rows // gz
    cuts_a = 2 if slots % 2 == 0 else 1
    dma = pltpu.SemaphoreType.DMA
    any_spec = pl.BlockSpec(memory_space=pl.ANY)
    smem_spec = pl.BlockSpec(memory_space=pltpu.SMEM)
    return pl.pallas_call(
        functools.partial(kernel, gx, gy, gz, slots_p),
        out_shape=jax.ShapeDtypeStruct((rows_out * tile, COLS_DEV * tile), jnp.float32),
        in_specs=[any_spec] * 2 + [smem_spec] * 4,
        out_specs=pl.BlockSpec(memory_space=pltpu.VMEM),
        scratch_shapes=[
            pltpu.VMEM((gx, rows, slots, tile, tile), jnp.float32),
            pltpu.VMEM((tiles_p, tile, tile), jnp.float32),
            pltpu.VMEM((gy, 2, pairs, tile, tile), jnp.float32),
            pltpu.VMEM((gx, 8, 128), jnp.int32),
            pltpu.VMEM((gy, 8, 128), jnp.int32),
            pltpu.SMEM((gx, 8, 128), jnp.int32),
            pltpu.SMEM((gy, 8, 128), jnp.int32),
            pltpu.VMEM((2, gy * inner + 1, tile, 2 * tile), jnp.bfloat16),
            pltpu.VMEM((gz, rows_out, 2, tile, tile), jnp.float32),
            pltpu.VMEM((gz, rows_out, 2, tile, tile), jnp.float32),
            dma((gx, rows, cuts_a)),
            dma((max(gx // 2, 1), rows, cuts_a)),
            dma((rows, cuts_a)),
            dma((max(gx // 2, 1), rows, cuts_a)),
            dma,
            dma((gy, 2, pairs)),
            dma((2, gy, 2, pairs)),
            dma((gx,)),
            dma((gx,)),
            dma((gy,)),
            dma((gy,)),
            dma((2,)),
            dma((gz, rows_out, 2)),
            dma((gz, rows_out, 2)),
        ],
        compiler_params=pltpu.CompilerParams(collective_id=0, has_side_effects=True),
    )(
        a_vals[0, :, 0], p_vals.reshape(tiles_p, tile, tile),
        a_cols, a_count.reshape(-1), p_cols.reshape(-1), p_count.reshape(-1),
    )


def solution(mesh):
    placed = (
        P("gy", "gx", "gz", None, None, None),
        P("gy", "gx", "gz", None),
        P("gy", "gx", "gz"),
        P("gz", "gy", "gx", None, None, None),
        P("gz", "gy", "gx", None),
        P("gz", "gy", "gx"),
    )
    sizes = (mesh.shape["gx"], mesh.shape["gy"], mesh.shape["gz"])
    return jax.shard_map(
        functools.partial(body, *sizes),
        mesh=mesh, in_specs=placed, out_specs=P(("gy", "gz"), "gx"), check_vma=False,
    )
```

profile of v0, /device:TPU:4, one launch (start us, length us, event | category | flops | bytes accessed | tf_op | source)
XLA Modules:
  0.0 40.0 jit_solution(4808773853659401375)
XLA Ops:
  0.0 38.1 %shard_map.64 = f32[512,256]{1,0:T(8,128)} custom-call(f32[2,6,128,128]{3,2,1,0:T(8,128)} %bitcast.5, f32[4,128,128]{2,1,0:T(8,128)} %bitcast.6, s32[1,2,1,6]{3,2,1,0:T(1,128)} %ac_ref.1, s32[2]{0:T(128)} %bitcast.7, s32[4]{0:T(128)} %bitcast.8, s32[4]{0:T(128)} %bitcast.9), custom_call_target="tpu_custom_call" | custom-call | tf_op jit(solution)/shard_map/pallas_call | solution.py:301
  38.2 1.9 %copy.8 = f32[512,256]{1,0:T(8,128)} copy(f32[512,256]{1,0:T(8,128)} %shard_map.64) | data formatting | bytes 1048576
where the time goes:
time: 40.3 us; the launch traced here: 40 us
  Pallas kernels  38.1 us (95%)
  local copies, waits for them, and re-layouts  1.87 us (5%)
    pallas_call x1, Pallas kernels, body(): pl.pallas_call(functools.partial(kernel, gx, gy, gz, slots_p), out_shape=...  38.1 us
    unnamed x1, local copies, waits for them, and re-layouts  1.87 us

commit v1 on v0

v1 whole, which is shorter than its diff:
```python
import functools

import jax
import jax.numpy as jnp
from jax import lax
from jax.experimental import pallas as pl
from jax.experimental.pallas import tpu as pltpu
from jax.sharding import PartitionSpec as P

COLS_DEV = 2
CUTS = 4
MESH = pl.DeviceIdType.MESH


def plan(gy):
    if gy == 4:
        opening = [(1, 0), (1, 1), (2, 1), (2, 0)]
        stages = [
            [("fwd", 0, 1, 0), ("fwd", 0, 1, 1)],
            [("fwd", 1, 1, 0), ("fwd", 1, 1, 1), ("own", 3, 0, 0), ("own", 3, 0, 1)],
            [("fwd", 2, 1, 0), ("fwd", 0, 2, 1)],
            [("fwd", 3, 1, 0), ("fwd", 1, 2, 1), ("fwd", 2, 1, 1)],
            [("fwd", 2, 2, 1), ("fwd", 3, 1, 1)],
            [("fwd", 3, 2, 1)],
        ]
        return opening, stages
    opening = [(q, rel) for q in range(1, CUTS) for rel in (0, 1)]
    waves = [[("fwd", q, d, rel) for d in range(1, gy) for rel in (0, 1)] for q in range(CUTS)]
    return opening, [[], [], waves[0], waves[1], waves[2], waves[3]]


def kernel(
    gx, gy, gz, slots_p, tiles_p,
    a_ref, p_ref, ac_ref, an_ref, pc_ref, pn_ref, o_ref,
    a_all, a_hl, p_own, p_all, ma, sa, p_mul, c_send, c_recv,
    a_recv, a_sy, a_sp, a_sf, p_load, p_recv, p_send,
    ma_recv, ma_send, s_sem, c_rs, c_ss,
):
    rows, slots, tile = a_ref.shape[0], a_ref.shape[1], a_ref.shape[2]
    blocks = p_all.shape[1]
    head = 8
    inner = tiles_p // slots_p
    rows_out = gx * rows // gz
    zero_tile = gy * inner
    width = tile // CUTS
    half = tile // 2
    part = slots // 2
    opening, stages = plan(gy)
    chips = gx // 2
    far = chips - 1
    me_x, me_y, me_z = lax.axis_index("gx"), lax.axis_index("gy"), lax.axis_index("gz")
    chip, core = me_x // 2, me_x % 2
    partner = chip * 2 + (1 - core)
    has_next = (me_y + 1 < gy, me_y >= 1)

    def remote(src, dst, send, recv, where):
        return pltpu.make_async_remote_copy(
            src_ref=src, dst_ref=dst, send_sem=send, recv_sem=recv,
            device_id=where, device_id_type=MESH)

    def arrive(ref, sem):
        pltpu.make_async_copy(ref, ref, sem).wait()

    barrier = pltpu.get_barrier_semaphore()
    for name, size, me in (("gx", gx, me_x), ("gz", gz, me_z)):
        for d in range(1, size):
            pl.semaphore_signal(
                barrier, inc=1, device_id={name: lax.rem(me + d, size)}, device_id_type=MESH
            )
    for side, step in ((0, 1), (1, -1)):
        @pl.when(has_next[side])
        def _(step=step):
            pl.semaphore_signal(
                barrier, inc=1, device_id={"gy": lax.rem(me_y + step + gy, gy)},
                device_id_type=MESH)

    load = pltpu.make_async_copy(p_ref, p_own, p_load)
    load.start()

    def a_piece(g, r, h):
        return a_all.at[g, r, pl.ds(h * part, part)]

    own_loads = []
    for r in range(rows):
        for h in (0, 1):
            own_loads.append(pltpu.make_async_copy(
                a_ref.at[r, pl.ds(h * part, part)], a_piece(me_x, r, h), a_recv.at[me_x, r, h]))
    for copy in own_loads:
        copy.start()

    line = lax.broadcasted_iota(jnp.int32, (8, 128), 0)
    lane = lax.broadcasted_iota(jnp.int32, (8, 128), 1)
    meta = jnp.zeros((8, 128), jnp.int32)
    for r in range(rows):
        for s in range(slots):
            pick = jnp.where(s < an_ref[r], ac_ref[0, r, 0, s], zero_tile)
            meta = jnp.where((line == 0) & (lane == r * slots + s), pick, meta)
    ma[me_x] = meta
    group = lax.broadcasted_iota(jnp.int32, (tile, tile), 1) // width
    group8 = lax.broadcasted_iota(jnp.int32, (8, tile), 1) // width
    for q in range(CUTS // 2):
        p_mul[q, zero_tile] = jnp.zeros_like(p_mul[q, zero_tile])

    load.wait()
    for b in range(blocks):
        mine = [b * CUTS + t for t in range(CUTS) if b * CUTS + t < tiles_p]
        code = jnp.full((8, tile), -1.0, jnp.float32)
        for n, t in enumerate(mine):
            kind = jnp.where(t % slots_p < pn_ref[t // slots_p], pc_ref[t], -1)
            code = jnp.where(group8 == n, kind.astype(jnp.float32), code)
        for q in range(CUTS):
            value = jnp.zeros((tile, tile), jnp.float32)
            for n, t in enumerate(mine):
                shift = (n - q) % CUTS * width
                turned = pltpu.roll(p_own[t], shift, 1) if shift else p_own[t]
                value = jnp.where(group == n, turned, value)
            p_all[me_y, b, head + q * tile:head + (q + 1) * tile] = value
        p_all[me_y, b, :head] = code
    for r in range(rows):
        for h in (0, 1):
            arrive(a_piece(me_x, r, h), a_recv.at[me_x, r, h])

    neighbours = jnp.where(has_next[0], 1, 0) + jnp.where(has_next[1], 1, 0)
    pl.semaphore_wait(barrier, gx + gz - 2 + neighbours)

    def p_block(src, q, b):
        if q == 0:
            return p_all.at[src, b, pl.ds(0, head + tile)]
        return p_all.at[src, b, pl.ds(head + q * tile, tile)]

    def p_copy(side, src, q, b):
        ref = p_block(src, q, b)
        step = 1 if side == 0 else -1
        return remote(ref, ref, p_send.at[side, src, q, b], p_recv.at[src, q, b],
                      {"gy": lax.rem(me_y + step + gy, gy)})

    near_side = jnp.where(2 * me_y < gy - 1, 0, 1)

    def on_side(side, rel):
        return near_side == side if rel == 0 else near_side != side

    def send_own(q, rel):
        for side in (0, 1):
            @pl.when(jnp.logical_and(on_side(side, rel), has_next[side]))
            def _(side=side):
                for b in range(blocks):
                    p_copy(side, me_y, q, b).start()

    sends = []

    def send(copy):
        copy.start()
        sends.append(copy)

    def cross(d):
        return {"gx": lax.rem(chip + d, chips) * 2 + core}

    for d in range(1, gx):
        send(remote(ma.at[me_x], ma.at[me_x], ma_send.at[d], ma_recv.at[me_x],
                    {"gx": lax.rem(me_x + d, gx)}))
    for rel in (0, 1):
        send_own(0, rel)
    for h in (0, 1):
        for d in range(1, chips):
            send(remote(a_piece(me_x, 0, h), a_piece(me_x, 0, h), a_sy.at[d, 0, h],
                        a_recv.at[me_x, 0, h], cross(d)))
    for r in list(range(1, rows)) + [0]:
        for h in (0, 1):
            send(remote(a_piece(me_x, r, h), a_piece(me_x, r, h), a_sp.at[r, h],
                        a_recv.at[me_x, r, h], {"gx": partner}))
    for q, rel in opening:
        send_own(q, rel)

    def prepare(g, r):
        values = jnp.concatenate([a_all[g, r, s] for s in range(slots)], axis=1)
        high = values.astype(jnp.bfloat16)
        a_hl[g, r, :tile] = high
        a_hl[g, r, tile:] = (values - high.astype(jnp.float32)).astype(jnp.bfloat16)

    def unpack_one(src, q):
        value = jnp.zeros((tile, tile), jnp.float32)
        for b in range(blocks):
            packed = p_all[src, b, head + q * tile:head + (q + 1) * tile]
            code = p_all[src, b, :head]
            high = packed.astype(jnp.bfloat16).astype(jnp.float32)
            low = packed - high
            turn = lambda x: [x] + [pltpu.roll(x, s * width, 1) for s in range(1, CUTS)]
            highs, lows, codes = turn(high), turn(low), turn(code)
            for n in range(CUTS):
                t = b * CUTS + n
                if t >= tiles_p:
                    continue
                parts = [highs[-n % CUTS], highs[(1 - n) % CUTS],
                         lows[(2 - n) % CUTS], lows[(3 - n) % CUTS]]
                kinds = [codes[(p - n) % CUTS] for p in range(CUTS)]
                chosen, kind = parts[3], kinds[3]
                for p in (2, 1, 0):
                    chosen = jnp.where(group == p, parts[p], chosen)
                    kind = jnp.where(group8 == p, kinds[p], kind)
                want = (group8 % COLS_DEV).astype(jnp.float32)
                keep = jnp.where(kind == want, 1.0, 0.0)
                keep = jnp.concatenate([keep] * (tile // 8), axis=0)
                placed = jnp.where(keep > 0.5, chosen, 0.0)
                value = placed if t % slots_p == 0 else value + placed
                if t % slots_p == slots_p - 1:
                    side = q % 2 * tile
                    p_mul[q // 2, src * inner + t // slots_p, :, side:side + tile] = (
                        value.astype(jnp.bfloat16))

    def source(side, d):
        src = me_y - d if side == 0 else me_y + d
        return src, src >= 0 if side == 0 else src < gy

    def forward(q, d, rel):
        for side in (0, 1):
            src, there = source(side, d)

            @pl.when(jnp.logical_and(on_side(side, rel), jnp.logical_and(there, has_next[side])))
            def _(src=src, side=side):
                for b in range(blocks):
                    arrive(p_block(src, q, b), p_recv.at[src, q, b])
                    p_copy(side, src, q, b).start()

    def advance(n):
        for kind, q, d, rel in stages[n]:
            if kind == "own":
                send_own(q, rel)
            else:
                forward(q, d, rel)

    def unpack(q):
        for d in range(1, gy):
            for side in (0, 1):
                src, there = source(side, d)

                @pl.when(there)
                def _(src=src, side=side):
                    @pl.when(jnp.logical_not(has_next[side]))
                    def _():
                        for b in range(blocks):
                            arrive(p_block(src, q, b), p_recv.at[src, q, b])
                    unpack_one(src, q)

    def chip_at(d):
        return lax.rem(chip + d, chips)

    def piece_of(g, r, h):
        return a_piece(g, r, h), a_recv.at[g, r, h]

    def relay_copies(r, o):
        copies = []
        for d in range(1, chips):
            came = lax.rem(chip - d + chips, chips)
            if r == 0:
                g, h = came * 2 + core, o
            else:
                g, h = came * 2 + o, core
            ref, sem = piece_of(g, r, h)
            copies.append((ref, sem, remote(ref, ref, a_sf.at[d, r, o], sem, {"gx": partner})))
        return copies

    def relay(r, o):
        for ref, sem, copy in relay_copies(r, o):
            arrive(ref, sem)
            copy.start()

    lanes = lax.broadcasted_iota(jnp.int32, (half, tile), 1)

    def product(g, r, cuts):
        picks = [sa[g, 0, r * slots + s] for s in range(slots)]
        first = cuts[0] % 2 * tile
        span = pl.ds(first, len(cuts) * tile)
        right = jnp.concatenate([p_mul[cuts[0] // 2, i, :, span] for i in picks], axis=0)
        out = jnp.dot(a_hl[g, r], right, preferred_element_type=jnp.float32)
        results = []
        for n in range(len(cuts)):
            both = out[:tile, n * tile:(n + 1) * tile] + out[tile:, n * tile:(n + 1) * tile]
            both = both + pltpu.roll(both, half, 1)
            results.append(jnp.where(lanes < half, both[:half], both[half:]))
        return results

    def c_copy(z, i, q):
        return remote(c_send.at[z, i, q], c_recv.at[me_z, i, q], c_ss.at[z, i, q],
                      c_rs.at[me_z, i, q], {"gz": z})

    def emit(spots, cuts):
        results = []
        for group_of in cuts:
            results += [(g, r, group_of, product(g, r, group_of)) for g, r in spots]
        for g, r, group_of, values in results:
            at = g * rows + r
            z, i = at // rows_out, lax.rem(at, rows_out)
            for q, value in zip(group_of, values):
                c_send[z, i, q] = value

            @pl.when(z != me_z)
            def _():
                for q in group_of:
                    c_copy(z, i, q).start()

    def near_row(n):
        return chip * 2 + n // rows, lax.rem(n, rows)

    def far_row(n):
        r = n // (2 * far)
        o = lax.rem(n // far, 2)
        return chip_at(1 + lax.rem(n, far)) * 2 + o, r

    n_near, n_far = 2 * rows, 2 * rows * far

    def near(q):
        emit([near_row(n) for n in range(n_near)], ((q,),))

    def far_rows(r, sides, cuts):
        for d in range(1, chips):
            emit([(chip_at(d) * 2 + o, r) for o in sides], cuts)

    def prepare_far(r, o):
        for d in range(1, chips):
            g = chip_at(d) * 2 + o
            for h in (0, 1):
                if r == 0:
                    direct = core == o
                else:
                    direct = core == h

                @pl.when(jnp.logical_not(direct))
                def _(g=g, h=h):
                    arrive(*piece_of(g, r, h))
            prepare(g, r)

    for r in range(rows):
        prepare(me_x, r)
    for r in list(range(1, rows)) + [0]:
        for h in (0, 1):
            arrive(*piece_of(partner, r, h))
    for r in range(1, rows):
        for o in (0, 1):
            for d in range(1, chips):
                ref, sem = piece_of(chip * 2 + o, r, core)
                send(remote(ref, ref, a_sy.at[d, r, o], sem, cross(d)))
    for q in range(CUTS):
        unpack_one(me_y, q)
    for d in range(1, gx):
        g = lax.rem(me_x + d, gx)
        arrive(ma.at[g], ma_recv.at[g])
    move = pltpu.make_async_copy(ma, sa, s_sem)
    move.start()
    for r in range(rows):
        prepare(partner, r)
    move.wait()

    last = n_far - far
    advance(0)
    advance(1)
    relay(0, 0)
    advance(2)
    unpack(0)
    near(0)
    advance(3)
    relay(0, 1)
    unpack(1)
    near(1)
    prepare_far(0, 0)
    prepare_far(0, 1)
    advance(4)
    far_rows(0, (0, 1), ((0, 1),))
    advance(5)
    for r in range(1, rows):
        for o in (0, 1):
            if (r, o) != (rows - 1, 1):
                relay(r, o)
                prepare_far(r, o)
                far_rows(r, (o,), ((0, 1),))
    unpack(2)
    near(2)
    far_rows(0, (0, 1), ((2,),))
    for r in range(1, rows):
        for o in (0, 1):
            if (r, o) != (rows - 1, 1):
                far_rows(r, (o,), ((2,),))
    unpack(3)
    near_mine = (chip * n_near) // rows_out == me_z
    total = n_near + (last if rows > 1 else n_far)
    begin = jnp.where(near_mine, n_near, 0)

    def mixed(n):
        m = lax.rem(n + begin, total)
        is_near = m < n_near
        g0, r0 = near_row(m)
        g1, r1 = far_row(jnp.maximum(m - n_near, 0)) if far else (g0, r0)
        return jnp.where(is_near, g0, g1), jnp.where(is_near, r0, r1)

    early = min(3, total)
    emit([mixed(n) for n in range(early)], ((3,),))
    if rows > 1:
        relay(rows - 1, 1)
    emit([mixed(n) for n in range(early, total)], ((3,),))
    if rows > 1:
        prepare_far(rows - 1, 1)
        far_rows(rows - 1, (1,), ((0, 1), (2, 3)))

    def finish(i):
        top = [None, None]
        low = [None, None]
        spot = lanes // width
        for q in range(CUTS):
            value = c_send[me_z, i, q]
            for d in range(1, gz):
                z = lax.rem(me_z + d, gz)
                arrive(c_recv.at[z, i, q], c_rs.at[z, i, q])
                value = value + c_recv[z, i, q]
            turned = [value] + [pltpu.roll(value, s * width, 1) for s in range(1, CUTS)]
            for c in range(COLS_DEV):
                for store, base in ((top, c), (low, c + COLS_DEV)):
                    piece = turned[(q - base) % CUTS]
                    store[c] = piece if q == 0 else jnp.where(spot == q, piece, store[c])
        for c in range(COLS_DEV):
            o_ref[pl.ds(i * tile, half), c * tile:(c + 1) * tile] = top[c]
            o_ref[pl.ds(i * tile + half, half), c * tile:(c + 1) * tile] = low[c]

    for r in range(rows):
        for i in range(r, rows_out, rows):
            finish(i)

    for copy in sends:
        copy.wait_send()
    for r in range(rows):
        for o in (0, 1):
            for _, _, copy in relay_copies(r, o):
                copy.wait_send()
    for side in (0, 1):
        for d in range(0, gy):
            src, there = source(side, d)

            @pl.when(jnp.logical_and(there, has_next[side]))
            def _(src=src, side=side):
                for q in range(CUTS):
                    for b in range(blocks):
                        p_copy(side, src, q, b).wait_send()
    for d in range(1, gz):
        z = lax.rem(me_z + d, gz)
        for i in range(rows_out):
            for q in range(CUTS):
                c_copy(z, i, q).wait_send()


def body(gx, gy, gz, a_vals, a_cols, a_count, p_vals, p_cols, p_count):
    if a_vals.shape[3] % 2:
        wide = [(0, 0)] * 3 + [(0, 1)]
        a_vals = jnp.pad(a_vals, wide + [(0, 0)] * 2)
        a_cols = jnp.pad(a_cols, wide)
    rows, slots, tile = a_vals.shape[1], a_vals.shape[3], a_vals.shape[-1]
    inner, slots_p = p_vals.shape[1], p_vals.shape[3]
    tiles_p = inner * slots_p
    blocks = -(-tiles_p // CUTS)
    rows_out = gx * rows // gz
    chips = max(gx // 2, 1)
    dma = pltpu.SemaphoreType.DMA
    any_spec = pl.BlockSpec(memory_space=pl.ANY)
    smem_spec = pl.BlockSpec(memory_space=pltpu.SMEM)
    return pl.pallas_call(
        functools.partial(kernel, gx, gy, gz, slots_p, tiles_p),
        out_shape=pltpu.VMEM((rows_out * tile, COLS_DEV * tile), jnp.float32),
        in_specs=[any_spec] * 2 + [smem_spec] * 4,
        out_specs=pl.BlockSpec(memory_space=pltpu.VMEM),
        scratch_shapes=[
            pltpu.VMEM((gx, rows, slots, tile, tile), jnp.float32),
            pltpu.VMEM((gx, rows, 2 * tile, slots * tile), jnp.bfloat16),
            pltpu.VMEM((tiles_p, tile, tile), jnp.float32),
            pltpu.VMEM((gy, blocks, 8 + CUTS * tile, tile), jnp.float32),
            pltpu.VMEM((gx, 8, 128), jnp.int32),
            pltpu.SMEM((gx, 8, 128), jnp.int32),
            pltpu.VMEM((CUTS // 2, gy * inner + 1, tile, 2 * tile), jnp.bfloat16),
            pltpu.VMEM((gz, rows_out, CUTS, tile // 2, tile), jnp.float32),
            pltpu.VMEM((gz, rows_out, CUTS, tile // 2, tile), jnp.float32),
            dma((gx, rows, 2)),
            dma((chips, rows, 2)),
            dma((rows, 2)),
            dma((chips, rows, 2)),
            dma,
            dma((gy, CUTS, blocks)),
            dma((2, gy, CUTS, blocks)),
            dma((gx,)),
            dma((gx,)),
            dma,
            dma((gz, rows_out, CUTS)),
            dma((gz, rows_out, CUTS)),
        ],
        compiler_params=pltpu.CompilerParams(collective_id=0, has_side_effects=True),
    )(
        a_vals[0, :, 0], p_vals.reshape(tiles_p, tile, tile),
        a_cols, a_count.reshape(-1), p_cols.reshape(-1), p_count.reshape(-1),
    )


def solution(mesh):
    placed = (
        P("gy", "gx", "gz", None, None, None),
        P("gy", "gx", "gz", None),
        P("gy", "gx", "gz"),
        P("gz", "gy", "gx", None, None, None),
        P("gz", "gy", "gx", None),
        P("gz", "gy", "gx"),
    )
    sizes = (mesh.shape["gx"], mesh.shape["gy"], mesh.shape["gz"])
    return jax.shard_map(
        functools.partial(body, *sizes),
        mesh=mesh, in_specs=placed, out_specs=P(("gy", "gz"), "gx"), check_vma=False,
    )
```

time: 40.3 us -> 35.2 us (0.87)
  Pallas kernels: 38.1 us -> 34.3 us
  local copies, waits for them, and re-layouts: 1.87 us -> 0.8 us
    pallas_call x1, Pallas kernels: 38.1 us -> 34.3 us  [body(): pl.pallas_call(functools.partial(kernel, gx, gy, gz, slots_p, tiles_p), o...]
    unnamed x1, local copies, waits for them, and re-layouts: 1.87 us -> 0.8 us
where the time goes in v1:
time: 35.2 us; the launch traced here: 35.1 us
  Pallas kernels  34.3 us (97%)
  local copies, waits for them, and re-layouts  0.8 us (2%)
    pallas_call x1, Pallas kernels, body(): pl.pallas_call(functools.partial(kernel, gx, gy, gz, slots_p, tiles_p), o...  34.3 us
    unnamed x1, local copies, waits for them, and re-layouts  0.8 us

profile of v1, /device:TPU:4, one launch (start us, length us, event | category | flops | bytes accessed | tf_op | source)
XLA Modules:
  0.0 35.1 jit_solution(17269172905028318760)
XLA Ops:
  0.0 34.3 %shard_map.64 = f32[512,256]{1,0:T(8,128)S(1)} custom-call(f32[2,6,128,128]{3,2,1,0:T(8,128)} %bitcast.5, f32[4,128,128]{2,1,0:T(8,128)} %bitcast.6, s32[1,2,1,6]{3,2,1,0:T(1,128)} %ac_ref.1, s32[2]{0:T(128)} %bitcast.7, s32[4]{0:T(128)} %bitcast.8, s32[4]{0:T(128)} %bitcast.9), custom_call_target="tpu_custom_call" | custom-call | tf_op jit(solution)/shard_map/pallas_call | solution.py:462
  34.3 0.8 %copy.8 = f32[512,256]{1,0:T(8,128)} copy(f32[512,256]{1,0:T(8,128)S(1)} %shard_map.64) | data formatting | bytes 1048576

commit v2 on v1

v2 whole, which is shorter than its diff:
```python
import functools

import jax
import jax.numpy as jnp
from jax import lax
from jax.experimental import pallas as pl
from jax.experimental.pallas import tpu as pltpu
from jax.sharding import PartitionSpec as P

COLS_DEV = 2
CUTS = 4
MESH = pl.DeviceIdType.MESH


def plan(gy):
    if gy == 4:
        opening = [(1, 0), (1, 1), (2, 1), (2, 0)]
        stages = [
            [("fwd", 0, 1, 1), ("fwd", 0, 1, 0)],
            [("fwd", 1, 1, 1), ("fwd", 1, 1, 0)],
            [("fwd", 2, 1, 0), ("fwd", 2, 1, 1), ("mid", 3, 0, 0), ("mid", 3, 0, 1)],
            [("fwd", 3, 1, 0)],
            [("fwd", 2, 2, 1), ("fwd", 3, 1, 1)],
            [("fwd", 3, 2, 1)],
        ]
        return opening, stages, 2
    opening = [(q, rel) for q in range(1, CUTS) for rel in (0, 1)]
    waves = [[("fwd", q, d, rel) for d in range(1, gy) for rel in (0, 1)] for q in range(CUTS)]
    return opening, [[], [], waves[0], waves[1], waves[2], waves[3]], 0


def kernel(
    gx, gy, gz, slots_p, tiles_p,
    a_ref, p_ref, ac_ref, an_ref, pc_ref, pn_ref, o_ref,
    a_all, a_hl, p_own, p_all, ma, sa, p_mul, c_send, c_recv,
    a_recv, a_sy, a_sp, a_sf, p_load, p_recv, p_send,
    ma_recv, ma_send, s_sem, c_rs, c_ss, far_ok, far_send,
):
    rows, slots, tile = a_ref.shape[0], a_ref.shape[1], a_ref.shape[2]
    blocks = p_all.shape[1]
    head = 8
    inner = tiles_p // slots_p
    rows_out = gx * rows // gz
    zero_tile = gy * inner
    width = tile // CUTS
    half = tile // 2
    quarter = half // 2
    part = slots // 2
    opening, stages, straight = plan(gy)
    chips = gx // 2
    far = chips - 1
    me_x, me_y, me_z = lax.axis_index("gx"), lax.axis_index("gy"), lax.axis_index("gz")
    chip, core = me_x // 2, me_x % 2
    partner = chip * 2 + (1 - core)
    has_next = (me_y + 1 < gy, me_y >= 1)

    def remote(src, dst, send, recv, where):
        return pltpu.make_async_remote_copy(
            src_ref=src, dst_ref=dst, send_sem=send, recv_sem=recv,
            device_id=where, device_id_type=MESH)

    def arrive(ref, sem):
        pltpu.make_async_copy(ref, ref, sem).wait()

    barrier = pltpu.get_barrier_semaphore()
    for name, size, me in (("gx", gx, me_x), ("gz", gz, me_z)):
        for d in range(1, size):
            pl.semaphore_signal(
                barrier, inc=1, device_id={name: lax.rem(me + d, size)}, device_id_type=MESH
            )
    for side, step in ((0, 1), (1, -1)):
        @pl.when(has_next[side])
        def _(step=step):
            pl.semaphore_signal(
                barrier, inc=1, device_id={"gy": lax.rem(me_y + step + gy, gy)},
                device_id_type=MESH)

    load = pltpu.make_async_copy(p_ref, p_own, p_load)
    load.start()

    def a_piece(g, r, h, v):
        at = pl.ds(v * half, half)
        if r == 0:
            return a_all.at[g, 0, :, at], a_recv.at[g, v]
        return (a_all.at[g, r, pl.ds(h * part, part), at],
                a_recv.at[g, 2 + (r - 1) * 4 + h * 2 + v])

    own_loads = [pltpu.make_async_copy(a_ref.at[r], a_all.at[me_x, r], a_recv.at[me_x, r])
                 for r in range(rows)]
    for copy in own_loads:
        copy.start()

    line = lax.broadcasted_iota(jnp.int32, (8, 128), 0)
    lane = lax.broadcasted_iota(jnp.int32, (8, 128), 1)
    meta = jnp.zeros((8, 128), jnp.int32)
    for r in range(rows):
        for s in range(slots):
            pick = jnp.where(s < an_ref[r], ac_ref[0, r, 0, s], zero_tile)
            meta = jnp.where((line == 0) & (lane == r * slots + s), pick, meta)
    ma[me_x] = meta
    group = lax.broadcasted_iota(jnp.int32, (tile, tile), 1) // width
    group8 = lax.broadcasted_iota(jnp.int32, (8, tile), 1) // width
    for q in range(CUTS // 2):
        p_mul[q, zero_tile] = jnp.zeros_like(p_mul[q, zero_tile])

    load.wait()
    for b in range(blocks):
        mine = [b * CUTS + t for t in range(CUTS) if b * CUTS + t < tiles_p]
        code = jnp.full((8, tile), -1.0, jnp.float32)
        for n, t in enumerate(mine):
            kind = jnp.where(t % slots_p < pn_ref[t // slots_p], pc_ref[t], -1)
            code = jnp.where(group8 == n, kind.astype(jnp.float32), code)
        for q in range(CUTS):
            value = jnp.zeros((tile, tile), jnp.float32)
            for n, t in enumerate(mine):
                shift = (n - q) % CUTS * width
                turned = pltpu.roll(p_own[t], shift, 1) if shift else p_own[t]
                value = jnp.where(group == n, turned, value)
            p_all[me_y, b, head + q * tile:head + (q + 1) * tile] = value
        p_all[me_y, b, :head] = code
    for r in range(rows):
        arrive(a_all.at[me_x, r], a_recv.at[me_x, r])

    neighbours = jnp.where(has_next[0], 1, 0) + jnp.where(has_next[1], 1, 0)
    pl.semaphore_wait(barrier, gx + gz - 2 + neighbours)

    def p_block(src, q, b):
        if q == 0:
            return p_all.at[src, b, pl.ds(0, head + tile)]
        return p_all.at[src, b, pl.ds(head + q * tile, tile)]

    def p_copy(side, src, q, b):
        ref = p_block(src, q, b)
        step = 1 if side == 0 else -1
        return remote(ref, ref, p_send.at[side, src], p_recv.at[src, q, b],
                      {"gy": lax.rem(me_y + step + gy, gy)})

    near_side = jnp.where(2 * me_y < gy - 1, 0, 1)

    def on_side(side, rel):
        return near_side == side if rel == 0 else near_side != side

    def send_own(q, rel, only=True):
        for side in (0, 1):
            @pl.when(jnp.logical_and(only, jnp.logical_and(on_side(side, rel), has_next[side])))
            def _(side=side):
                for b in range(blocks):
                    p_copy(side, me_y, q, b).start()

    between = jnp.logical_and(has_next[0], has_next[1])
    onward = jnp.where(near_side == 0, 1, -1)

    def tell(step):
        pl.semaphore_signal(far_ok, inc=1, device_id={"gy": me_y + step}, device_id_type=MESH)

    if straight:
        @pl.when(between)
        def _():
            tell(onward)

    def send(copy):
        copy.start()

    def cross(d):
        return {"gx": lax.rem(chip + d, chips) * 2 + core}

    for d in range(1, gx):
        send(remote(ma.at[me_x], ma.at[me_x], ma_send, ma_recv,
                    {"gx": lax.rem(me_x + d, gx)}))
    for rel in (0, 1):
        send_own(0, rel)
    for v in (0, 1):
        for d in range(1, chips):
            ref, sem = a_piece(me_x, 0, 0, v)
            send(remote(ref, ref, a_sy.at[d], sem, cross(d)))
    for r in list(range(1, rows)) + [0]:
        send(remote(a_all.at[me_x, r], a_all.at[me_x, r], a_sp,
                    a_recv.at[me_x, r], {"gx": partner}))
    for q, rel in opening:
        send_own(q, rel)

    def prepare(g, r, v):
        at = pl.ds(v * half, half)
        values = jnp.concatenate([a_all[g, r, s, at] for s in range(slots)], axis=1)
        high = values.astype(jnp.bfloat16)
        a_hl[g, r, v * half:(v + 1) * half] = high
        low = (values - high.astype(jnp.float32)).astype(jnp.bfloat16)
        a_hl[g, r, tile + v * half:tile + (v + 1) * half] = low

    def unpack_one(src, q):
        value = jnp.zeros((tile, tile), jnp.float32)
        for b in range(blocks):
            packed = p_all[src, b, head + q * tile:head + (q + 1) * tile]
            code = p_all[src, b, :head]
            high = packed.astype(jnp.bfloat16).astype(jnp.float32)
            low = packed - high
            turn = lambda x: [x] + [pltpu.roll(x, s * width, 1) for s in range(1, CUTS)]
            highs, lows, codes = turn(high), turn(low), turn(code)
            for n in range(CUTS):
                t = b * CUTS + n
                if t >= tiles_p:
                    continue
                parts = [highs[-n % CUTS], highs[(1 - n) % CUTS],
                         lows[(2 - n) % CUTS], lows[(3 - n) % CUTS]]
                kinds = [codes[(p - n) % CUTS] for p in range(CUTS)]
                chosen, kind = parts[3], kinds[3]
                for p in (2, 1, 0):
                    chosen = jnp.where(group == p, parts[p], chosen)
                    kind = jnp.where(group8 == p, kinds[p], kind)
                want = (group8 % COLS_DEV).astype(jnp.float32)
                keep = jnp.where(kind == want, 1.0, 0.0)
                keep = jnp.concatenate([keep] * (tile // 8), axis=0)
                placed = jnp.where(keep > 0.5, chosen, 0.0)
                value = placed if t % slots_p == 0 else value + placed
                if t % slots_p == slots_p - 1:
                    side = q % 2 * tile
                    p_mul[q // 2, src * inner + t // slots_p, :, side:side + tile] = (
                        value.astype(jnp.bfloat16))

    def source(side, d):
        src = me_y - d if side == 0 else me_y + d
        return src, src >= 0 if side == 0 else src < gy

    def forward(q, d, rel):
        for side in (0, 1):
            src, there = source(side, d)

            @pl.when(jnp.logical_and(on_side(side, rel), jnp.logical_and(there, has_next[side])))
            def _(src=src, side=side):
                for b in range(blocks):
                    arrive(p_block(src, q, b), p_recv.at[src, q, b])
                    p_copy(side, src, q, b).start()

    def advance(n):
        for kind, q, d, rel in stages[n]:
            if kind == "own":
                send_own(q, rel)
            elif kind == "mid":
                send_own(q, rel, between)
            else:
                forward(q, d, rel)

    def unpack(q):
        for d in range(1, gy):
            for side in (0, 1):
                src, there = source(side, d)

                @pl.when(there)
                def _(src=src, side=side):
                    loose = q < straight and d == 2

                    @pl.when(True if loose else jnp.logical_not(has_next[side]))
                    def _():
                        for b in range(blocks):
                            arrive(p_block(src, q, b), p_recv.at[src, q, b])
                    unpack_one(src, q)

    def chip_at(d):
        return lax.rem(chip + d, chips)

    def relay_copies(r, o, v):
        copies = []
        for d in range(1, chips):
            came = lax.rem(chip - d + chips, chips)
            g = came * 2 + (core if r == 0 else o)
            ref, sem = a_piece(g, r, core, v)
            copies.append((ref, sem, remote(
                ref, ref, a_sf.at[d], sem, {"gx": partner})))
        return copies

    def relay(r, o, v):
        for ref, sem, copy in relay_copies(r, o, v):
            arrive(ref, sem)
            copy.start()

    lane_id = lax.broadcasted_iota(jnp.int32, (quarter, tile), 1)

    def product(g, r, v, cuts):
        picks = [sa[g, 0, r * slots + s] for s in range(slots)]
        first = cuts[0] % 2 * tile
        span = pl.ds(first, len(cuts) * tile)
        right = jnp.concatenate([p_mul[cuts[0] // 2, i, :, span] for i in picks], axis=0)
        if v is None:
            left, size = a_hl[g, r], tile
        else:
            left, size = jnp.concatenate(
                [a_hl[g, r, pl.ds(b + v * half, half)] for b in (0, tile)], axis=0), half
        out = jnp.dot(left, right, preferred_element_type=jnp.float32)
        results = []
        for n in range(len(cuts)):
            both = out[:size, n * tile:(n + 1) * tile] + out[size:, n * tile:(n + 1) * tile]
            both = both + pltpu.roll(both, half, 1)
            results.append(jnp.concatenate(
                [jnp.where(lane_id < half, both[b:b + quarter], both[b + quarter:b + half])
                 for b in range(0, size, half)], axis=0))
        return results

    def c_copy(z, i, q, v=None):
        at = pl.ds(0, half) if v is None else pl.ds(v * quarter, quarter)
        return remote(c_send.at[z, i, q, at], c_recv.at[me_z, i, q, at], c_ss.at[z],
                      c_rs.at[lax.rem(me_z - z - 1 + 2 * gz, gz), i, q // (CUTS - 1)], {"gz": z})

    def emit(spots, cuts):
        results = []
        for group_of in cuts:
            results += [(g, r, v, group_of, product(g, r, v, group_of)) for g, r, v in spots]
        for g, r, v, group_of, values in results:
            at = g * rows + r
            z, i = at // rows_out, lax.rem(at, rows_out)
            for q, value in zip(group_of, values):
                if v is None:
                    c_send[z, i, q] = value
                else:
                    c_send[z, i, q, v * quarter:(v + 1) * quarter] = value

            @pl.when(z != me_z)
            def _():
                for q in group_of:
                    c_copy(z, i, q, v).start()

    def near_row(n):
        return chip * 2 + n // rows, lax.rem(n, rows)

    def far_row(n):
        r = n // (2 * far)
        o = lax.rem(n // far, 2)
        return chip_at(1 + lax.rem(n, far)) * 2 + o, r

    n_near, n_far = 2 * rows, 2 * rows * far

    def near(q):
        emit([near_row(n) + (None,) for n in range(n_near)], ((q,),))

    def far_rows(r, sides, v, cuts):
        for d in range(1, chips):
            emit([(chip_at(d) * 2 + o, r, v) for o in sides], cuts)

    def prepare_far(r, sides, v):
        for d in range(1, chips):
            for o in sides:
                g = chip_at(d) * 2 + o
                for h in (0,) if r == 0 else (0, 1):
                    direct = core == (o if r == 0 else h)

                    @pl.when(jnp.logical_not(direct))
                    def _(g=g, h=h):
                        arrive(*a_piece(g, r, h, v))
                prepare(g, r, v)

    for r in range(rows):
        for v in (0, 1):
            prepare(me_x, r, v)
    if straight:
        @pl.when(between)
        def _():
            pl.semaphore_wait(far_ok, 1)
            tell(-onward)
    for r in list(range(1, rows)) + [0]:
        arrive(a_all.at[partner, r], a_recv.at[partner, r])
    for r in range(1, rows):
        for o in (0, 1):
            for v in (0, 1):
                for d in range(1, chips):
                    ref, sem = a_piece(chip * 2 + o, r, core, v)
                    send(remote(ref, ref, a_sy.at[d], sem, cross(d)))
    if straight:
        @pl.when(jnp.logical_not(between))
        def _():
            pl.semaphore_wait(far_ok, 1)
            for q in range(straight):
                for b in range(blocks):
                    ref = p_block(me_y, q, b)
                    remote(ref, ref, far_send, p_recv.at[me_y, q, b],
                           {"gy": gy - 1 - me_y}).start()
            send_own(CUTS - 1, 0)
    for q in range(CUTS):
        unpack_one(me_y, q)
    arrive(ma.at[pl.ds(0, gx - 1)], ma_recv)
    move = pltpu.make_async_copy(ma, sa, s_sem)
    move.start()
    for r in range(rows):
        for v in (0, 1):
            prepare(partner, r, v)
    move.wait()

    last_row = (rows - 1, 1)
    middle = [(r, o) for r in range(1, rows) for o in (0, 1) if (r, o) != last_row]
    both = (0, 1)
    near_mine = (chip * n_near) // rows_out == me_z

    def all_rows(n_more):
        total = n_near + n_more
        begin = jnp.where(near_mine, n_near, 0)
        spots = []
        for n in range(total):
            m = lax.rem(n + begin, total)
            is_near = m < n_near
            g0, r0 = near_row(m)
            g1, r1 = far_row(jnp.maximum(m - n_near, 0)) if far else (g0, r0)
            spots.append((jnp.where(is_near, g0, g1), jnp.where(is_near, r0, r1), None))
        return spots

    def sweep(spots, q):
        for n in range(0, len(spots), 3):
            emit(spots[n:n + 3], ((q,),))

    n_first = 2 * far
    advance(0)
    advance(1)
    relay(0, 0, 0)
    advance(2)
    advance(3)
    prepare_far(0, both, 0)
    unpack(0)
    relay(0, 0, 1)
    far_rows(0, both, 0, ((0,),))
    near(0)
    unpack(1)
    far_rows(0, both, 0, ((1,),))
    near(1)
    advance(4)
    prepare_far(0, both, 1)
    far_rows(0, both, 1, ((0, 1),))
    for v in both:
        for r, o in middle:
            relay(r, o, v)
    advance(5)
    for v in both:
        for r, o in middle:
            prepare_far(r, (o,), v)
            far_rows(r, (o,), v, ((0, 1),))
    unpack(2)
    if rows > 1:
        relay(*last_row, 0)
    sweep(all_rows(n_far - far if rows > 1 else n_far), 2)
    unpack(3)
    spots = all_rows(n_far - far if rows > 1 else n_far)
    sweep(spots[:3], 3)
    if rows > 1:
        prepare_far(rows - 1, (1,), 0)
        relay(*last_row, 1)
        far_rows(rows - 1, (1,), 0, ((0, 1), (2, 3)))
    emit(spots[3:], ((3,),))
    if rows > 1:
        prepare_far(rows - 1, (1,), 1)
        far_rows(rows - 1, (1,), 1, ((0, 1), (2, 3)))

    lanes = lax.broadcasted_iota(jnp.int32, (half, tile), 1)

    spot = lanes // width

    def finish(n, cuts, fresh):
        i = jnp.where(near_mine, n, n % (rows_out // rows) * rows + n // (rows_out // rows))
        top = [None, None]
        low = [None, None]
        for d in range(1, gz):
            z = lax.rem(me_z + d, gz)
            arrive(c_recv.at[z, i, pl.ds(cuts[0], len(cuts))], c_rs.at[d - 1, i, 0 if fresh else 1])
        for q in cuts:
            value = c_send[me_z, i, q]
            for d in range(1, gz):
                value = value + c_recv[lax.rem(me_z + d, gz), i, q]
            turned = [value] + [pltpu.roll(value, s * width, 1) for s in range(1, CUTS)]
            for c in range(COLS_DEV):
                for store, base in ((top, c), (low, c + COLS_DEV)):
                    piece = turned[(q - base) % CUTS]
                    old = store[c]
                    store[c] = piece if old is None else jnp.where(spot == q, piece, old)
        ours = spot >= cuts[0]
        for c in range(COLS_DEV):
            lane_to = slice(c * tile, (c + 1) * tile)
            for b in (0, 1):
                for e, store in enumerate((top, low)):
                    to = pl.ds(pl.multiple_of(i * tile + b * half + e * quarter, quarter), quarter)
                    at = slice(b * quarter, (b + 1) * quarter)
                    value = store[c][at]
                    if not fresh:
                        value = jnp.where(ours[at], value, o_ref[to, lane_to])
                    o_ref[to, lane_to] = value

    for n in range(rows_out):
        finish(n, range(CUTS - 1), True)
    for n in range(rows_out):
        finish(n, (CUTS - 1,), False)

    arrive(ma.at[pl.ds(0, gx - 1)], ma_send)
    for d in range(1, chips):
        arrive(a_all.at[me_x], a_sy.at[d])
        arrive(a_all.at[me_x], a_sf.at[d])
    arrive(a_all.at[me_x], a_sp)
    for side in (0, 1):
        for d in range(0, gy):
            src, there = source(side, d)

            @pl.when(jnp.logical_and(there, has_next[side]))
            def _(src=src, side=side, d=d):
                skip = head + straight * tile if straight and d == 2 else 0
                ref = p_all.at[src, :, pl.ds(skip, head + CUTS * tile - skip)]
                arrive(ref, p_send.at[side, src])
    if straight:
        @pl.when(jnp.logical_not(between))
        def _():
            arrive(p_all.at[me_y, :, pl.ds(0, head + straight * tile)], far_send)
    for d in range(1, gz):
        z = lax.rem(me_z + d, gz)
        arrive(c_send.at[z], c_ss.at[z])


def body(gx, gy, gz, a_vals, a_cols, a_count, p_vals, p_cols, p_count):
    if a_vals.shape[3] % 2:
        wide = [(0, 0)] * 3 + [(0, 1)]
        a_vals = jnp.pad(a_vals, wide + [(0, 0)] * 2)
        a_cols = jnp.pad(a_cols, wide)
    rows, slots, tile = a_vals.shape[1], a_vals.shape[3], a_vals.shape[-1]
    inner, slots_p = p_vals.shape[1], p_vals.shape[3]
    tiles_p = inner * slots_p
    blocks = -(-tiles_p // CUTS)
    rows_out = gx * rows // gz
    chips = max(gx // 2, 1)
    dma = pltpu.SemaphoreType.DMA
    any_spec = pl.BlockSpec(memory_space=pl.ANY)
    smem_spec = pl.BlockSpec(memory_space=pltpu.SMEM)
    return pl.pallas_call(
        functools.partial(kernel, gx, gy, gz, slots_p, tiles_p),
        out_shape=pltpu.VMEM((rows_out * tile, COLS_DEV * tile), jnp.float32),
        in_specs=[any_spec] * 2 + [smem_spec] * 4,
        out_specs=pl.BlockSpec(memory_space=pltpu.VMEM),
        scratch_shapes=[
            pltpu.VMEM((gx, rows, slots, tile, tile), jnp.float32),
            pltpu.VMEM((gx, rows, 2 * tile, slots * tile), jnp.bfloat16),
            pltpu.VMEM((tiles_p, tile, tile), jnp.float32),
            pltpu.VMEM((gy, blocks, 8 + CUTS * tile, tile), jnp.float32),
            pltpu.VMEM((gx, 8, 128), jnp.int32),
            pltpu.SMEM((gx, 8, 128), jnp.int32),
            pltpu.VMEM((CUTS // 2, gy * inner + 1, tile, 2 * tile), jnp.bfloat16),
            pltpu.VMEM((gz, rows_out, CUTS, tile // 2, tile), jnp.float32),
            pltpu.VMEM((gz, rows_out, CUTS, tile // 2, tile), jnp.float32),
            dma((gx, max(4 * rows - 2, rows))),
            dma((chips,)),
            dma,
            dma((chips,)),
            dma,
            dma((gy, CUTS, blocks)),
            dma((2, gy)),
            dma,
            dma,
            dma,
            dma((max(gz - 1, 1), rows_out, 2)),
            dma((gz,)),
            pltpu.SemaphoreType.REGULAR,
            dma,
        ],
        compiler_params=pltpu.CompilerParams(collective_id=0, has_side_effects=True),
    )(
        a_vals[0, :, 0], p_vals.reshape(tiles_p, tile, tile),
        a_cols, a_count.reshape(-1), p_cols.reshape(-1), p_count.reshape(-1),
    )


def solution(mesh):
    placed = (
        P("gy", "gx", "gz", None, None, None),
        P("gy", "gx", "gz", None),
        P("gy", "gx", "gz"),
        P("gz", "gy", "gx", None, None, None),
        P("gz", "gy", "gx", None),
        P("gz", "gy", "gx"),
    )
    sizes = (mesh.shape["gx"], mesh.shape["gy"], mesh.shape["gz"])
    return jax.shard_map(
        functools.partial(body, *sizes),
        mesh=mesh, in_specs=placed, out_specs=P(("gy", "gz"), "gx"), check_vma=False,
    )
```

time: 35.2 us -> 32.7 us (0.929)
  the two profiles are of different devices: /device:TPU:4 before, /device:TPU:13 now
where the time goes in v2:
time: 32.7 us; the launch traced here: 32.6 us
  Pallas kernels  31.8 us (97%)
  local copies, waits for them, and re-layouts  0.8 us (2%)
    pallas_call x1, Pallas kernels, body(): pl.pallas_call(functools.partial(kernel, gx, gy, gz, slots_p, tiles_p), o...  31.8 us
    unnamed x1, local copies, waits for them, and re-layouts  0.8 us

profile of v2, /device:TPU:13, one launch (start us, length us, event | category | flops | bytes accessed | tf_op | source)
XLA Modules:
  0.0 32.6 jit_solution(517252259736148000)
XLA Ops:
  0.0 31.8 %shard_map.64 = f32[512,256]{1,0:T(8,128)S(1)} custom-call(f32[2,6,128,128]{3,2,1,0:T(8,128)} %bitcast.5, f32[4,128,128]{2,1,0:T(8,128)} %bitcast.6, s32[1,2,1,6]{3,2,1,0:T(1,128)} %ac_ref.1, s32[2]{0:T(128)} %bitcast.7, s32[4]{0:T(128)} %bitcast.8, s32[4]{0:T(128)} %bitcast.9), custom_call_target="tpu_custom_call" | custom-call | tf_op jit(solution)/shard_map/pallas_call | solution.py:523
  31.8 0.8 %copy.8 = f32[512,256]{1,0:T(8,128)} copy(f32[512,256]{1,0:T(8,128)S(1)} %shard_map.64) | data formatting | bytes 1048576

commit v3 on v2

--- a/solution.py
+++ b/solution.py
@@ -20,13 +20,14 @@
             [("fwd", 1, 1, 1), ("fwd", 1, 1, 0)],
             [("fwd", 2, 1, 0), ("fwd", 2, 1, 1), ("mid", 3, 0, 0), ("mid", 3, 0, 1)],
             [("fwd", 3, 1, 0)],
-            [("fwd", 2, 2, 1), ("fwd", 3, 1, 1)],
+            [("fwd", 2, 2, 1)],
+            [("fwd", 3, 1, 1)],
             [("fwd", 3, 2, 1)],
         ]
         return opening, stages, 2
     opening = [(q, rel) for q in range(1, CUTS) for rel in (0, 1)]
     waves = [[("fwd", q, d, rel) for d in range(1, gy) for rel in (0, 1)] for q in range(CUTS)]
-    return opening, [[], [], waves[0], waves[1], waves[2], waves[3]], 0
+    return opening, [[], [], waves[0], waves[1], waves[2], [], waves[3]], 0
 
 
 def kernel(
@@ -411,8 +412,8 @@
     advance(2)
     advance(3)
     prepare_far(0, both, 0)
+    relay(0, 0, 1)
     unpack(0)
-    relay(0, 0, 1)
     far_rows(0, both, 0, ((0,),))
     near(0)
     unpack(1)
@@ -421,26 +422,30 @@
     advance(4)
     prepare_far(0, both, 1)
     far_rows(0, both, 1, ((0, 1),))
-    for v in both:
-        for r, o in middle:
-            relay(r, o, v)
+    for r, o in middle:
+        relay(r, o, 0)
     advance(5)
-    for v in both:
-        for r, o in middle:
-            prepare_far(r, (o,), v)
-            far_rows(r, (o,), v, ((0, 1),))
+    for r, o in middle:
+        relay(r, o, 1)
+        prepare_far(r, (o,), 0)
+        far_rows(r, (o,), 0, ((0, 1),))
+    advance(6)
+    for r, o in middle:
+        prepare_far(r, (o,), 1)
+        far_rows(r, (o,), 1, ((0, 1),))
+    spots = all_rows(n_far - far if rows > 1 else n_far)
+    soon, later = spots[:n_near], spots[n_near:]
     unpack(2)
     if rows > 1:
         relay(*last_row, 0)
-    sweep(all_rows(n_far - far if rows > 1 else n_far), 2)
+    emit(soon, ((2,),))
     unpack(3)
-    spots = all_rows(n_far - far if rows > 1 else n_far)
-    sweep(spots[:3], 3)
+    emit(soon, ((3,),))
     if rows > 1:
         prepare_far(rows - 1, (1,), 0)
+        far_rows(rows - 1, (1,), 0, ((0, 1), (2, 3)))
         relay(*last_row, 1)
-        far_rows(rows - 1, (1,), 0, ((0, 1), (2, 3)))
-    emit(spots[3:], ((3,),))
+    emit(later, ((2, 3),))
     if rows > 1:
         prepare_far(rows - 1, (1,), 1)
         far_rows(rows - 1, (1,), 1, ((0, 1), (2, 3)))
@@ -478,10 +483,12 @@
                         value = jnp.where(ours[at], value, o_ref[to, lane_to])
                     o_ref[to, lane_to] = value
 
-    for n in range(rows_out):
-        finish(n, range(CUTS - 1), True)
-    for n in range(rows_out):
-        finish(n, (CUTS - 1,), False)
+    final = rows_out - 1
+    for spans in (range(final), range(final, rows_out)):
+        for n in spans:
+            finish(n, range(CUTS - 1), True)
+        for n in spans:
+            finish(n, (CUTS - 1,), False)
 
     arrive(ma.at[pl.ds(0, gx - 1)], ma_send)
     for d in range(1, chips):

time: 32.7 us -> 32 us (0.979)
  the two profiles are of different devices: /device:TPU:13 before, /device:TPU:4 now
where the time goes in v3:
time: 32 us; the launch traced here: 31.9 us
  Pallas kernels  31.1 us (97%)
  local copies, waits for them, and re-layouts  0.8 us (2%)
    pallas_call x1, Pallas kernels, body(): pl.pallas_call(functools.partial(kernel, gx, gy, gz, slots_p, tiles_p), o...  31.1 us
    unnamed x1, local copies, waits for them, and re-layouts  0.8 us

profile of v3, /device:TPU:4, one launch (start us, length us, event | category | flops | bytes accessed | tf_op | source)
XLA Modules:
  0.0 31.9 jit_solution(5245296793457342216)
XLA Ops:
  0.0 31.1 %shard_map.64 = f32[512,256]{1,0:T(8,128)S(1)} custom-call(f32[2,6,128,128]{3,2,1,0:T(8,128)} %bitcast.5, f32[4,128,128]{2,1,0:T(8,128)} %bitcast.6, s32[1,2,1,6]{3,2,1,0:T(1,128)} %ac_ref.1, s32[2]{0:T(128)} %bitcast.7, s32[4]{0:T(128)} %bitcast.8, s32[4]{0:T(128)} %bitcast.9), custom_call_target="tpu_custom_call" | custom-call | tf_op jit(solution)/shard_map/pallas_call | solution.py:530
  31.1 0.8 %copy.8 = f32[512,256]{1,0:T(8,128)} copy(f32[512,256]{1,0:T(8,128)S(1)} %shard_map.64) | data formatting | bytes 1048576

commit v4 on v3

--- a/solution.py
+++ b/solution.py
@@ -34,7 +34,7 @@
     gx, gy, gz, slots_p, tiles_p,
     a_ref, p_ref, ac_ref, an_ref, pc_ref, pn_ref, o_ref,
     a_all, a_hl, p_own, p_all, ma, sa, p_mul, c_send, c_recv,
-    a_recv, a_sy, a_sp, a_sf, p_load, p_recv, p_send,
+    a_recv, a_near, a_sy, a_sp, a_sf, p_load, p_recv, p_send,
     ma_recv, ma_send, s_sem, c_rs, c_ss, far_ok, far_send,
 ):
     rows, slots, tile = a_ref.shape[0], a_ref.shape[1], a_ref.shape[2]
@@ -79,14 +79,15 @@
     load = pltpu.make_async_copy(p_ref, p_own, p_load)
     load.start()
 
-    def a_piece(g, r, h, v):
+    def a_piece(g, r, h, v, gap):
         at = pl.ds(v * half, half)
+        spot = (gap - 1) * 2 + lax.rem(g, 2)
         if r == 0:
-            return a_all.at[g, 0, :, at], a_recv.at[g, v]
+            return a_all.at[g, 0, :, at], a_recv.at[spot, v]
         return (a_all.at[g, r, pl.ds(h * part, part), at],
-                a_recv.at[g, 2 + (r - 1) * 4 + h * 2 + v])
-
-    own_loads = [pltpu.make_async_copy(a_ref.at[r], a_all.at[me_x, r], a_recv.at[me_x, r])
+                a_recv.at[spot, 2 + (r - 1) * 4 + h * 2 + v])
+
+    own_loads = [pltpu.make_async_copy(a_ref.at[r], a_all.at[me_x, r], a_near.at[0])
                  for r in range(rows)]
     for copy in own_loads:
         copy.start()
@@ -119,8 +120,7 @@
                 value = jnp.where(group == n, turned, value)
             p_all[me_y, b, head + q * tile:head + (q + 1) * tile] = value
         p_all[me_y, b, :head] = code
-    for r in range(rows):
-        arrive(a_all.at[me_x, r], a_recv.at[me_x, r])
+    arrive(a_all.at[me_x], a_near.at[0])
 
     neighbours = jnp.where(has_next[0], 1, 0) + jnp.where(has_next[1], 1, 0)
     pl.semaphore_wait(barrier, gx + gz - 2 + neighbours)
@@ -133,7 +133,8 @@
     def p_copy(side, src, q, b):
         ref = p_block(src, q, b)
         step = 1 if side == 0 else -1
-        return remote(ref, ref, p_send.at[side, src], p_recv.at[src, q, b],
+        slot = gy if side == 0 and src is me_y else src
+        return remote(ref, ref, p_send.at[slot], p_recv.at[src, q, b],
                       {"gy": lax.rem(me_y + step + gy, gy)})
 
     near_side = jnp.where(2 * me_y < gy - 1, 0, 1)
@@ -172,11 +173,11 @@
         send_own(0, rel)
     for v in (0, 1):
         for d in range(1, chips):
-            ref, sem = a_piece(me_x, 0, 0, v)
-            send(remote(ref, ref, a_sy.at[d], sem, cross(d)))
+            ref, sem = a_piece(me_x, 0, 0, v, chips - d)
+            send(remote(ref, ref, a_sy.at[d - 1], sem, cross(d)))
     for r in list(range(1, rows)) + [0]:
         send(remote(a_all.at[me_x, r], a_all.at[me_x, r], a_sp,
-                    a_recv.at[me_x, r], {"gx": partner}))
+                    a_near.at[1], {"gx": partner}))
     for q, rel in opening:
         send_own(q, rel)
 
@@ -264,9 +265,9 @@
         for d in range(1, chips):
             came = lax.rem(chip - d + chips, chips)
             g = came * 2 + (core if r == 0 else o)
-            ref, sem = a_piece(g, r, core, v)
+            ref, sem = a_piece(g, r, core, v, chips - d)
             copies.append((ref, sem, remote(
-                ref, ref, a_sf.at[d], sem, {"gx": partner})))
+                ref, ref, a_sf.at[d - 1], sem, {"gx": partner})))
         return copies
 
     def relay(r, o, v):
@@ -344,8 +345,8 @@
                     direct = core == (o if r == 0 else h)
 
                     @pl.when(jnp.logical_not(direct))
-                    def _(g=g, h=h):
-                        arrive(*a_piece(g, r, h, v))
+                    def _(g=g, h=h, d=d):
+                        arrive(*a_piece(g, r, h, v, d))
                 prepare(g, r, v)
 
     for r in range(rows):
@@ -356,14 +357,13 @@
         def _():
             pl.semaphore_wait(far_ok, 1)
             tell(-onward)
-    for r in list(range(1, rows)) + [0]:
-        arrive(a_all.at[partner, r], a_recv.at[partner, r])
+    arrive(a_all.at[partner], a_near.at[1])
     for r in range(1, rows):
         for o in (0, 1):
             for v in (0, 1):
                 for d in range(1, chips):
-                    ref, sem = a_piece(chip * 2 + o, r, core, v)
-                    send(remote(ref, ref, a_sy.at[d], sem, cross(d)))
+                    ref, sem = a_piece(chip * 2 + o, r, core, v, chips - d)
+                    send(remote(ref, ref, a_sy.at[d - 1], sem, cross(d)))
     if straight:
         @pl.when(jnp.logical_not(between))
         def _():
@@ -492,8 +492,8 @@
 
     arrive(ma.at[pl.ds(0, gx - 1)], ma_send)
     for d in range(1, chips):
-        arrive(a_all.at[me_x], a_sy.at[d])
-        arrive(a_all.at[me_x], a_sf.at[d])
+        arrive(a_all.at[me_x], a_sy.at[d - 1])
+        arrive(a_all.at[me_x], a_sf.at[d - 1])
     arrive(a_all.at[me_x], a_sp)
     for side in (0, 1):
         for d in range(0, gy):
@@ -503,7 +503,7 @@
             def _(src=src, side=side, d=d):
                 skip = head + straight * tile if straight and d == 2 else 0
                 ref = p_all.at[src, :, pl.ds(skip, head + CUTS * tile - skip)]
-                arrive(ref, p_send.at[side, src])
+                arrive(ref, p_send.at[gy if side == 0 and d == 0 else src])
     if straight:
         @pl.when(jnp.logical_not(between))
         def _():
@@ -542,13 +542,14 @@
             pltpu.VMEM((CUTS // 2, gy * inner + 1, tile, 2 * tile), jnp.bfloat16),
             pltpu.VMEM((gz, rows_out, CUTS, tile // 2, tile), jnp.float32),
             pltpu.VMEM((gz, rows_out, CUTS, tile // 2, tile), jnp.float32),
-            dma((gx, max(4 * rows - 2, rows))),
-            dma((chips,)),
+            dma((max(2 * chips - 2, 1), max(4 * rows - 2, 2))),
+            dma((2,)),
+            dma((max(chips - 1, 1),)),
             dma,
-            dma((chips,)),
+            dma((max(chips - 1, 1),)),
             dma,
             dma((gy, CUTS, blocks)),
-            dma((2, gy)),
+            dma((gy + 1,)),
             dma,
             dma,
             dma,

time: 32 us -> 31.9 us (level)
  no operation moved by 1% of the time
where the time goes in v4:
time: 31.9 us; the launch traced here: 31.7 us
  Pallas kernels  30.9 us (97%)
  local copies, waits for them, and re-layouts  0.8 us (3%)
    pallas_call x1, Pallas kernels, body(): pl.pallas_call(functools.partial(kernel, gx, gy, gz, slots_p, tiles_p), o...  30.9 us
    unnamed x1, local copies, waits for them, and re-layouts  0.8 us

profile of v4, /device:TPU:4, one launch (start us, length us, event | category | flops | bytes accessed | tf_op | source)
XLA Modules:
  0.0 31.7 jit_solution(11837104951906339925)
XLA Ops:
  0.0 30.9 %shard_map.64 = f32[512,256]{1,0:T(8,128)S(1)} custom-call(f32[2,6,128,128]{3,2,1,0:T(8,128)} %bitcast.5, f32[4,128,128]{2,1,0:T(8,128)} %bitcast.6, s32[1,2,1,6]{3,2,1,0:T(1,128)} %ac_ref.1, s32[2]{0:T(128)} %bitcast.7, s32[4]{0:T(128)} %bitcast.8, s32[4]{0:T(128)} %bitcast.9), custom_call_target="tpu_custom_call" | custom-call | tf_op jit(solution)/shard_map/pallas_call | solution.py:530
  30.9 0.8 %copy.8 = f32[512,256]{1,0:T(8,128)} copy(f32[512,256]{1,0:T(8,128)S(1)} %shard_map.64) | data formatting | bytes 1048576
